TPU v7x, 256 devices: a whole 4x4x8 slice. The times are simulated.
256 devices in a mesh: grp: 8 (over z), sp: 32 (over y, x, core).
Axes of the slice: x: 4, y: 4, z: 8, core: 2. Of those that a mesh axis runs over, the one named last changes fastest.
Arguments:
- tokens: bfloat16 [16384, 2880], P(('grp', 'sp')), may hold values from -36 to 36
- query_weight: bfloat16 [2880, 2048], P(None, 'sp'), may hold values from -0.109375 to 0.109375
- key_value_weight: bfloat16 [2880, 1024], replicated, may hold values from -0.109375 to 0.109375
- block_places: int32 [32], replicated, may hold values from 0 to 31, each once
- sinks: float32 [32], replicated, may hold values from -1 to 5
Outputs:
- attended: bfloat16 [16384, 2048], P(('grp', 'sp'))
Inputs may be any that keep to these rules, and one draw needn't show every extreme that they name: `block_places`: every sequence block appears once.
All inputs are finite; a program needn't handle non-finite values.
Results may differ from a plain program's by a relative error of at most 0.008.
The roundings to bfloat16 on the way count: a program that leaves them out, or rounds other values in their place, can miss the bound.
Values may be sent and summed in bfloat16 or wider, within the bound.
A program may use at most 128 MiB of HBM per device.

v0:
```python
import jax
import jax.numpy as jnp
from jax import lax
from jax.sharding import PartitionSpec as P

QUERY_HEADS = 32
HEAD_SIZE = 64
BPG = 4
rope_base = 150000.0
neg_large = -1e30


def joined_along(pieces, dim):
    pieces = jnp.moveaxis(pieces, 0, dim)
    shape = pieces.shape
    return pieces.reshape(*shape[:dim], shape[dim] * shape[dim + 1], *shape[dim + 2 :])


def piecewise(value, axis, dim, apply, out_dim):
    size, span = (lax.axis_size(axis), value.shape[dim])
    count = 2 if span % 2 == 0 else 1
    finished, length = ([], span // count)
    for k in range(count):
        share = lax.slice_in_dim(value, k * length, (k + 1) * length, axis=dim)
        starts = jnp.arange(size) * span + k * length
        finished.append(jax.vmap(apply)(lax.all_gather(share, axis), starts))
    return joined_along(jnp.concatenate(finished, axis=out_dim + 1), out_dim)


def rotate(vectors, angles):
    middle = vectors.shape[-1] // 2
    first_half = vectors[..., :middle]
    second_half = vectors[..., middle:]
    cosine = jnp.cos(angles)
    sine_part = jnp.sin(angles)
    return jnp.concatenate(
        [
            first_half * cosine - second_half * sine_part,
            second_half * cosine + first_half * sine_part,
        ],
        axis=-1,
    )


def locate(stored, block_rows, block_places):
    blocks = stored // block_rows
    table = jnp.arange(block_places.shape[0], dtype=jnp.int32)
    onehot = (blocks[:, None] == table[None, :]).astype(jnp.int32)
    return jnp.sum(onehot * block_places[None, :], axis=1) * block_rows + stored % block_rows


def prepare(projected, own_places, query_cols, kv_cols, head_count):
    row_count = projected.shape[0]
    inverse = rope_base ** (-(jnp.arange(HEAD_SIZE // 2, dtype=jnp.float32) * 2.0) / HEAD_SIZE)
    angles = own_places.astype(jnp.float32)[:, None, None] * inverse[None, None, :]
    queries = rotate(
        projected[:, :query_cols].reshape(row_count, query_cols // HEAD_SIZE, HEAD_SIZE), angles
    ).astype(jnp.bfloat16)
    rotated_keys = rotate(
        projected[:, query_cols : query_cols + kv_cols].reshape(row_count, head_count, HEAD_SIZE),
        angles,
    )
    key_value_pair = jnp.concatenate(
        [rotated_keys.reshape(row_count, kv_cols), projected[:, query_cols + kv_cols :]], axis=1
    ).astype(jnp.bfloat16)
    return (queries, key_value_pair)


def attend(state, queries, query_places, key_value_pair, key_places, head_count):
    maxima, totals, mixture = state
    key_count = key_value_pair.shape[0]
    column_half = key_value_pair.shape[1] // 2
    key_part = key_value_pair[:, :column_half].reshape(key_count, head_count, HEAD_SIZE)
    value_part = key_value_pair[:, column_half:].reshape(key_count, head_count, HEAD_SIZE)
    scores = jnp.einsum(
        "qhgd,khd->hgqk", queries, key_part, preferred_element_type=jnp.float32
    ) * HEAD_SIZE ** (-0.5)
    allowed = key_places[None, :] <= query_places[:, None]
    scores = jnp.where(allowed, scores, neg_large)
    updated = jnp.maximum(maxima, jnp.max(scores, axis=-1))
    weights = jnp.where(allowed, jnp.exp(scores - updated[..., None]), 0.0)
    factor = jnp.exp(maxima - updated)
    totals = totals * factor + jnp.sum(weights, axis=-1)
    mixture = mixture * factor[..., None] + jnp.einsum(
        "hgqk,khd->hgqd",
        weights.astype(jnp.bfloat16),
        value_part,
        preferred_element_type=jnp.float32,
    )
    return (updated, totals, mixture)


def per_device(tokens, query_weight, key_value_weight, block_places, sinks):
    sp_count = lax.axis_size("sp")
    local_rows = tokens.shape[0]
    group_rows = local_rows * sp_count
    block_rows = group_rows // BPG
    kv_total = key_value_weight.shape[1] // (2 * HEAD_SIZE)
    sp_place = lax.axis_index("sp")
    grp_place = lax.axis_index("grp")
    query_cols = query_weight.shape[1]
    query_heads = query_cols // HEAD_SIZE
    head_count = max(kv_total // sp_count, 1)
    kv_cols = head_count * HEAD_SIZE
    first_head = sp_place * query_heads // (QUERY_HEADS // kv_total)
    key_weight = lax.dynamic_slice_in_dim(key_value_weight, first_head * HEAD_SIZE, kv_cols, 1)
    value_weight = lax.dynamic_slice_in_dim(
        key_value_weight, kv_total * HEAD_SIZE + first_head * HEAD_SIZE, kv_cols, 1
    )
    joined = jnp.concatenate([query_weight, key_weight, value_weight], axis=1)

    def project(piece, start):
        return jnp.dot(piece, joined, preferred_element_type=jnp.float32)

    projected = piecewise(tokens, "sp", 0, project, 0)
    query_local = jnp.arange(group_rows, dtype=jnp.int32)
    head_first = sp_place * query_heads
    own_places = locate(grp_place * group_rows + query_local, block_rows, block_places)
    queries, key_value_pair = prepare(projected, own_places, query_cols, kv_cols, head_count)
    query_sharing = query_heads // head_count
    head_sinks = lax.dynamic_slice_in_dim(sinks, head_first, query_heads, 0).reshape(
        head_count, query_sharing
    )
    sink_rows = jnp.broadcast_to(head_sinks[:, :, None], (head_count, query_sharing, group_rows))
    query_block4 = queries.reshape(group_rows, head_count, query_sharing, HEAD_SIZE)
    initial = (
        sink_rows,
        jnp.ones((head_count, query_sharing, group_rows), jnp.float32),
        jnp.zeros((head_count, query_sharing, group_rows, HEAD_SIZE), jnp.float32),
    )
    piece = lax.all_gather(key_value_pair, "grp", axis=0, tiled=True)
    step_rows = min(piece.shape[0], group_rows)
    turns = piece.shape[0] // step_rows

    def visit(turn, inner):
        offset = turn * step_rows
        piece_rows = lax.dynamic_slice_in_dim(piece, offset, step_rows, 0)
        position = offset + jnp.arange(step_rows, dtype=jnp.int32)
        stored = position // group_rows * group_rows + position % group_rows
        key_places = locate(stored, block_rows, block_places)
        return attend(inner, query_block4, own_places, piece_rows, key_places, head_count)

    maxima, totals, mixture = lax.fori_loop(0, turns, visit, initial)
    normed = jnp.transpose(mixture, (2, 0, 1, 3)) / jnp.transpose(totals, (2, 0, 1))[..., None]
    attended = normed.reshape(group_rows, query_cols).astype(jnp.bfloat16)
    return lax.all_to_all(attended, "sp", split_axis=0, concat_axis=1, tiled=True)


def solution(mesh):
    in_specs = (P(("grp", "sp"), None), P(None, "sp"), P(), P(), P())
    out_specs = P(("grp", "sp"), None)
    return jax.shard_map(
        per_device, mesh=mesh, in_specs=in_specs, out_specs=out_specs, check_vma=False
    )
```

profile of v0, /device:TPU:1, one launch (start us, length us, event | category | flops | bytes accessed | tf_op | source)
XLA Modules:
  0.0 353.2 jit_solution(3869679549317436455)
XLA Ops:
  11.8 55.8 %all-gather.8.cloned.1.call-done = bf16[1024,2880]{1,0:T(8,128)(2,1)} async-done(((bf16[32,2880]{1,0:T(8,128)(2,1)}), bf16[1024,2880]{1,0:T(8,128)(2,1)}) %all-gather.8.cloned.1.call-update) | async-done | bytes 5898256 | tf_op jit(solution)/shard_map/all_gather | solution.py:26
  67.6 4.5 %convolution_bitcast_fusion.1 = f32[32,32,192]{2,1,0:T(8,128)S(1)} fusion(bf16[32,32,2880]{2,1,0:T(8,128)(2,1)} %bitcast.94, bf16[2880,64]{0,1:T(8,128)(2,1)S(1)} %copy.44, bf16[2880,64]{0,1:T(8,128)(2,1)S(1)} %copy.43, bf16[2880,64]{0,1:T(8,128)(2,1)S(1)} %copy-done.2), kind=kOutput, calls=%fused_computation.49 | convolution fusion | flops 1135779840 | bytes 7790592 | tf_op jit(solution)/shard_map/vmap()/dot_general | solution.py:113
  72.1 50.5 %all-gather.10.cloned.1.call-done = bf16[1024,2880]{1,0:T(8,128)(2,1)} async-done(((bf16[32,2880]{1,0:T(8,128)(2,1)}), bf16[1024,2880]{1,0:T(8,128)(2,1)}) %all-gather.10.cloned.1.call-update) | async-done | bytes 5898256 | tf_op jit(solution)/shard_map/all_gather | solution.py:26
  122.6 4.5 %convolution_bitcast_fusion = f32[32,32,192]{2,1,0:T(8,128)S(1)} fusion(bf16[32,32,2880]{2,1,0:T(8,128)(2,1)} %bitcast.95, bf16[2880,64]{0,1:T(8,128)(2,1)S(1)} %copy.44, bf16[2880,64]{0,1:T(8,128)(2,1)S(1)} %copy.43, bf16[2880,64]{0,1:T(8,128)(2,1)S(1)} %copy-done.2), kind=kOutput, calls=%fused_computation.48 | convolution fusion | flops 1135779840 | bytes 7790592 | tf_op jit(solution)/shard_map/vmap()/dot_general | solution.py:113
  131.3 52.6 %all-gather.6.cloned.1.call-done = bf16[16384,128]{0,1:T(8,128)(2,1)} async-done(((bf16[2048,128]{0,1:T(8,128)(2,1)}), bf16[16384,128]{0,1:T(8,128)(2,1)}) %all-gather.6.cloned.1.call-update) | async-done | bytes 4194320 | tf_op jit(solution)/shard_map/all_gather | solution.py:131
  184.5 141.5 %while.21 = (s32[]{:T(128)}, f32[1,1,2048]{2,1,0:T(1,128)S(1)}, f32[1,1,2048]{2,1,0:T(1,128)S(1)}, f32[1,1,2048,64]{2,3,1,0:T(8,128)S(1)}, s32[32]{0:T(128)S(1)}...) while((s32[]{:T(128)}, f32[1,1,2048]{2,1,0:T(1,128)S(1)}, ...), condition=%wide.region_5.6_spmd.clone, body=%wide.region_1.5_spmd.clone.sunk | while | flops 1141592064 | bytes 119497064 | solution.py:143
  188.3 5.3 %fusion.75 = f32[2048]{0:T(1024)S(1)} fusion(f32[2048,2048]{1,0:T(8,128)S(1)} %get-tuple-element.393, f32[2048]{0:T(1024)S(1)} %bitcast.86, s32[2048]{0:T(1024)S(1)} %get-tuple-element.427, s32[2048]{0:T(1024)S(1)} %fusion.73), kind=kLoop, calls=%fused_computation.4.clone.1 | loop fusion | flops 25163776 | bytes 16809984 | tf_op jit(solution)/shard_map/while/body/eval_jaxpr/reduce_sum | solution.py:83
  194.1 8.1 %fusion.77 = f32[1,1,2048,64]{2,3,1,0:T(8,128)S(1)} fusion(f32[2048,2048]{1,0:T(8,128)} %copy-done, f32[2048]{0:T(1024)S(1)} %bitcast.87, s32[2048]{0:T(1024)S(1)} %get-tuple-element.427, s32[2048]{0:T(1024)S(1)} %fusion.73, f32[1,1,2048,64]{2,3,1,0:T(8,128)S(1)} %get-tuple-element.412, bf16[16384,128]{0,1:T(8,128)(2,1)} %get-tuple-element.428, ...), kind=kOutput, calls=%fused_computation.8.clone.1 | convolution fusion | flops 562429952 | bytes 18120712 | tf_op jit(solution)/shard_map/while/body/eval_jaxpr/hgqk,khd->hgqd/dot_general | solution.py:84
  202.4 3.6 %fusion.74 = (f32[2048]{0:T(1024)S(1)}, f32[2048,2048]{1,0:T(8,128)S(1)}) fusion(s32[2048]{0:T(1024)S(1)} %get-tuple-element.427, s32[2048]{0:T(1024)S(1)} %fusion.73, bf16[2048,1,1,64]{0,3,2,1:T(8,128)(2,1)S(1)} %get-tuple-element.429, bf16[16384,128]{0,1:T(8,128)(2,1)} %get-tuple-element.428, s32[]{:T(128)S(6)} %select_n.248), kind=kOutput, calls=%fused_computation.2.clone.1 | convolution fusion | flops 553646080 | bytes 17326084 | tf_op jit(solution)/shard_map/while/body/eval_jaxpr/qhgd,khd->hgqk/dot_general | solution.py:75
  206.0 5.3 %fusion.75 = f32[2048]{0:T(1024)S(1)} fusion(f32[2048,2048]{1,0:T(8,128)S(1)} %get-tuple-element.393, f32[2048]{0:T(1024)S(1)} %bitcast.86, s32[2048]{0:T(1024)S(1)} %get-tuple-element.427, s32[2048]{0:T(1024)S(1)} %fusion.73), kind=kLoop, calls=%fused_computation.4.clone.1 | loop fusion | flops 25163776 | bytes 16809984 | tf_op jit(solution)/shard_map/while/body/eval_jaxpr/reduce_sum | solution.py:83
  211.8 8.1 %fusion.77 = f32[1,1,2048,64]{2,3,1,0:T(8,128)S(1)} fusion(f32[2048,2048]{1,0:T(8,128)} %copy-done, f32[2048]{0:T(1024)S(1)} %bitcast.87, s32[2048]{0:T(1024)S(1)} %get-tuple-element.427, s32[2048]{0:T(1024)S(1)} %fusion.73, f32[1,1,2048,64]{2,3,1,0:T(8,128)S(1)} %get-tuple-element.412, bf16[16384,128]{0,1:T(8,128)(2,1)} %get-tuple-element.428, ...), kind=kOutput, calls=%fused_computation.8.clone.1 | convolution fusion | flops 562429952 | bytes 18120712 | tf_op jit(solution)/shard_map/while/body/eval_jaxpr/hgqk,khd->hgqd/dot_general | solution.py:84
  223.7 5.3 %fusion.75 = f32[2048]{0:T(1024)S(1)} fusion(f32[2048,2048]{1,0:T(8,128)S(1)} %get-tuple-element.393, f32[2048]{0:T(1024)S(1)} %bitcast.86, s32[2048]{0:T(1024)S(1)} %get-tuple-element.427, s32[2048]{0:T(1024)S(1)} %fusion.73), kind=kLoop, calls=%fused_computation.4.clone.1 | loop fusion | flops 25163776 | bytes 16809984 | tf_op jit(solution)/shard_map/while/body/eval_jaxpr/reduce_sum | solution.py:83
  229.5 8.1 %fusion.77 = f32[1,1,2048,64]{2,3,1,0:T(8,128)S(1)} fusion(f32[2048,2048]{1,0:T(8,128)} %copy-done, f32[2048]{0:T(1024)S(1)} %bitcast.87, s32[2048]{0:T(1024)S(1)} %get-tuple-element.427, s32[2048]{0:T(1024)S(1)} %fusion.73, f32[1,1,2048,64]{2,3,1,0:T(8,128)S(1)} %get-tuple-element.412, bf16[16384,128]{0,1:T(8,128)(2,1)} %get-tuple-element.428, ...), kind=kOutput, calls=%fused_computation.8.clone.1 | convolution fusion | flops 562429952 | bytes 18120712 | tf_op jit(solution)/shard_map/while/body/eval_jaxpr/hgqk,khd->hgqd/dot_general | solution.py:84
  241.4 5.3 %fusion.75 = f32[2048]{0:T(1024)S(1)} fusion(f32[2048,2048]{1,0:T(8,128)S(1)} %get-tuple-element.393, f32[2048]{0:T(1024)S(1)} %bitcast.86, s32[2048]{0:T(1024)S(1)} %get-tuple-element.427, s32[2048]{0:T(1024)S(1)} %fusion.73), kind=kLoop, calls=%fused_computation.4.clone.1 | loop fusion | flops 25163776 | bytes 16809984 | tf_op jit(solution)/shard_map/while/body/eval_jaxpr/reduce_sum | solution.py:83
  247.1 8.1 %fusion.77 = f32[1,1,2048,64]{2,3,1,0:T(8,128)S(1)} fusion(f32[2048,2048]{1,0:T(8,128)} %copy-done, f32[2048]{0:T(1024)S(1)} %bitcast.87, s32[2048]{0:T(1024)S(1)} %get-tuple-element.427, s32[2048]{0:T(1024)S(1)} %fusion.73, f32[1,1,2048,64]{2,3,1,0:T(8,128)S(1)} %get-tuple-element.412, bf16[16384,128]{0,1:T(8,128)(2,1)} %get-tuple-element.428, ...), kind=kOutput, calls=%fused_computation.8.clone.1 | convolution fusion | flops 562429952 | bytes 18120712 | tf_op jit(solution)/shard_map/while/body/eval_jaxpr/hgqk,khd->hgqd/dot_general | solution.py:84
  259.1 5.3 %fusion.75 = f32[2048]{0:T(1024)S(1)} fusion(f32[2048,2048]{1,0:T(8,128)S(1)} %get-tuple-element.393, f32[2048]{0:T(1024)S(1)} %bitcast.86, s32[2048]{0:T(1024)S(1)} %get-tuple-element.427, s32[2048]{0:T(1024)S(1)} %fusion.73), kind=kLoop, calls=%fused_computation.4.clone.1 | loop fusion | flops 25163776 | bytes 16809984 | tf_op jit(solution)/shard_map/while/body/eval_jaxpr/reduce_sum | solution.py:83
  264.8 8.1 %fusion.77 = f32[1,1,2048,64]{2,3,1,0:T(8,128)S(1)} fusion(f32[2048,2048]{1,0:T(8,128)} %copy-done, f32[2048]{0:T(1024)S(1)} %bitcast.87, s32[2048]{0:T(1024)S(1)} %get-tuple-element.427, s32[2048]{0:T(1024)S(1)} %fusion.73, f32[1,1,2048,64]{2,3,1,0:T(8,128)S(1)} %get-tuple-element.412, bf16[16384,128]{0,1:T(8,128)(2,1)} %get-tuple-element.428, ...), kind=kOutput, calls=%fused_computation.8.clone.1 | convolution fusion | flops 562429952 | bytes 18120712 | tf_op jit(solution)/shard_map/while/body/eval_jaxpr/hgqk,khd->hgqd/dot_general | solution.py:84
  276.8 5.3 %fusion.75 = f32[2048]{0:T(1024)S(1)} fusion(f32[2048,2048]{1,0:T(8,128)S(1)} %get-tuple-element.393, f32[2048]{0:T(1024)S(1)} %bitcast.86, s32[2048]{0:T(1024)S(1)} %get-tuple-element.427, s32[2048]{0:T(1024)S(1)} %fusion.73), kind=kLoop, calls=%fused_computation.4.clone.1 | loop fusion | flops 25163776 | bytes 16809984 | tf_op jit(solution)/shard_map/while/body/eval_jaxpr/reduce_sum | solution.py:83
  282.5 8.1 %fusion.77 = f32[1,1,2048,64]{2,3,1,0:T(8,128)S(1)} fusion(f32[2048,2048]{1,0:T(8,128)} %copy-done, f32[2048]{0:T(1024)S(1)} %bitcast.87, s32[2048]{0:T(1024)S(1)} %get-tuple-element.427, s32[2048]{0:T(1024)S(1)} %fusion.73, f32[1,1,2048,64]{2,3,1,0:T(8,128)S(1)} %get-tuple-element.412, bf16[16384,128]{0,1:T(8,128)(2,1)} %get-tuple-element.428, ...), kind=kOutput, calls=%fused_computation.8.clone.1 | convolution fusion | flops 562429952 | bytes 18120712 | tf_op jit(solution)/shard_map/while/body/eval_jaxpr/hgqk,khd->hgqd/dot_general | solution.py:84
  294.5 5.3 %fusion.75 = f32[2048]{0:T(1024)S(1)} fusion(f32[2048,2048]{1,0:T(8,128)S(1)} %get-tuple-element.393, f32[2048]{0:T(1024)S(1)} %bitcast.86, s32[2048]{0:T(1024)S(1)} %get-tuple-element.427, s32[2048]{0:T(1024)S(1)} %fusion.73), kind=kLoop, calls=%fused_computation.4.clone.1 | loop fusion | flops 25163776 | bytes 16809984 | tf_op jit(solution)/shard_map/while/body/eval_jaxpr/reduce_sum | solution.py:83
  300.2 8.1 %fusion.77 = f32[1,1,2048,64]{2,3,1,0:T(8,128)S(1)} fusion(f32[2048,2048]{1,0:T(8,128)} %copy-done, f32[2048]{0:T(1024)S(1)} %bitcast.87, s32[2048]{0:T(1024)S(1)} %get-tuple-element.427, s32[2048]{0:T(1024)S(1)} %fusion.73, f32[1,1,2048,64]{2,3,1,0:T(8,128)S(1)} %get-tuple-element.412, bf16[16384,128]{0,1:T(8,128)(2,1)} %get-tuple-element.428, ...), kind=kOutput, calls=%fused_computation.8.clone.1 | convolution fusion | flops 562429952 | bytes 18120712 | tf_op jit(solution)/shard_map/while/body/eval_jaxpr/hgqk,khd->hgqd/dot_general | solution.py:84
  312.2 5.3 %fusion.75 = f32[2048]{0:T(1024)S(1)} fusion(f32[2048,2048]{1,0:T(8,128)S(1)} %get-tuple-element.393, f32[2048]{0:T(1024)S(1)} %bitcast.86, s32[2048]{0:T(1024)S(1)} %get-tuple-element.427, s32[2048]{0:T(1024)S(1)} %fusion.73), kind=kLoop, calls=%fused_computation.4.clone.1 | loop fusion | flops 25163776 | bytes 16809984 | tf_op jit(solution)/shard_map/while/body/eval_jaxpr/reduce_sum | solution.py:83
  317.9 8.1 %fusion.77 = f32[1,1,2048,64]{2,3,1,0:T(8,128)S(1)} fusion(f32[2048,2048]{1,0:T(8,128)} %copy-done, f32[2048]{0:T(1024)S(1)} %bitcast.87, s32[2048]{0:T(1024)S(1)} %get-tuple-element.427, s32[2048]{0:T(1024)S(1)} %fusion.73, f32[1,1,2048,64]{2,3,1,0:T(8,128)S(1)} %get-tuple-element.412, bf16[16384,128]{0,1:T(8,128)(2,1)} %get-tuple-element.428, ...), kind=kOutput, calls=%fused_computation.8.clone.1 | convolution fusion | flops 562429952 | bytes 18120712 | tf_op jit(solution)/shard_map/while/body/eval_jaxpr/hgqk,khd->hgqd/dot_general | solution.py:84
  328.4 16.4 %all_to_all.16 = bf16[32,2,2048]{2,1,0:T(2,128)(2,1)S(1)} all-to-all(bf16[32,2,2048]{2,1,0:T(2,128)(2,1)S(1)} %reshape.437), channel_id=1, replica_groups=mesh['grp'=8,'sp'=32] {'sp'}, dimensions={0} | all-to-all | bytes 524288 | tf_op jit(solution)/shard_map/all_to_all | solution.py:146
  (114 shorter events, 43.9 us)
Async XLA Ops:
  6.5 5.1 %copy-start.1 = (s32[32]{0:T(128)S(1)}, s32[32]{0:T(128)}, u32[]{:S(2)}) copy-start(s32[32]{0:T(128)} %param.10) | copy-start | bytes 388
  6.5 61.1 %copy-start.2 = (bf16[2880,64]{0,1:T(8,128)(2,1)S(1)}, bf16[2880,64]{0,1:T(8,128)(2,1)}, u32[]{:S(2)}) copy-start(bf16[2880,64]{0,1:T(8,128)(2,1)} %param.8) | copy-start | bytes 1105924
  6.5 61.1 %all-gather.8.cloned.1.call-start = ((), (), s32[]{:S(2)}) async-start(), calls=%async_computation.2 | async-start | bytes 6217728 | tf_op jit(solution)/shard_map/all_gather | solution.py:26
  8.4 114.2 %all-gather.10.cloned.1.call-start = ((), (), s32[]{:S(2)}) async-start(), calls=%async_computation.3 | async-start | bytes 6217728 | tf_op jit(solution)/shard_map/all_gather | solution.py:26
  9.1 174.8 %all-gather.6.cloned.1.call-start = ((), (), s32[]{:S(2)}) async-start(), calls=%async_computation.1 | async-start | bytes 4718592 | tf_op jit(solution)/shard_map/all_gather | solution.py:131
  127.3 3.4 copy-start.3
  188.3 5.7 %copy-start = (f32[2048,2048]{1,0:T(8,128)}, f32[2048,2048]{1,0:T(8,128)S(1)}, u32[]{:S(2)}) copy-start(f32[2048,2048]{1,0:T(8,128)S(1)} %get-tuple-element.393) | copy-start | bytes 50331652 | tf_op jit(solution)/shard_map/while
  206.0 5.7 %copy-start = (f32[2048,2048]{1,0:T(8,128)}, f32[2048,2048]{1,0:T(8,128)S(1)}, u32[]{:S(2)}) copy-start(f32[2048,2048]{1,0:T(8,128)S(1)} %get-tuple-element.393) | copy-start | bytes 50331652 | tf_op jit(solution)/shard_map/while
  223.7 5.7 %copy-start = (f32[2048,2048]{1,0:T(8,128)}, f32[2048,2048]{1,0:T(8,128)S(1)}, u32[]{:S(2)}) copy-start(f32[2048,2048]{1,0:T(8,128)S(1)} %get-tuple-element.393) | copy-start | bytes 50331652 | tf_op jit(solution)/shard_map/while
  241.4 5.7 %copy-start = (f32[2048,2048]{1,0:T(8,128)}, f32[2048,2048]{1,0:T(8,128)S(1)}, u32[]{:S(2)}) copy-start(f32[2048,2048]{1,0:T(8,128)S(1)} %get-tuple-element.393) | copy-start | bytes 50331652 | tf_op jit(solution)/shard_map/while
  259.1 5.7 %copy-start = (f32[2048,2048]{1,0:T(8,128)}, f32[2048,2048]{1,0:T(8,128)S(1)}, u32[]{:S(2)}) copy-start(f32[2048,2048]{1,0:T(8,128)S(1)} %get-tuple-element.393) | copy-start | bytes 50331652 | tf_op jit(solution)/shard_map/while
  276.8 5.7 %copy-start = (f32[2048,2048]{1,0:T(8,128)}, f32[2048,2048]{1,0:T(8,128)S(1)}, u32[]{:S(2)}) copy-start(f32[2048,2048]{1,0:T(8,128)S(1)} %get-tuple-element.393) | copy-start | bytes 50331652 | tf_op jit(solution)/shard_map/while
  294.5 5.7 %copy-start = (f32[2048,2048]{1,0:T(8,128)}, f32[2048,2048]{1,0:T(8,128)S(1)}, u32[]{:S(2)}) copy-start(f32[2048,2048]{1,0:T(8,128)S(1)} %get-tuple-element.393) | copy-start | bytes 50331652 | tf_op jit(solution)/shard_map/while
  312.2 5.7 %copy-start = (f32[2048,2048]{1,0:T(8,128)}, f32[2048,2048]{1,0:T(8,128)S(1)}, u32[]{:S(2)}) copy-start(f32[2048,2048]{1,0:T(8,128)S(1)} %get-tuple-element.393) | copy-start | bytes 50331652 | tf_op jit(solution)/shard_map/while
Sparse Core Ops, SparseCore 0:
  9.9 57.7 all-gather.7
  70.2 52.4 all-gather.9
  130.8 53.0 all-gather.5
where the time goes:
time: 354 us; the launch traced here: 353 us
  waiting for transfers between devices  160 us (45%)
  matrix products  103 us (29%)
  other arithmetic  47.6 us (13%)
  blocking collectives  16.4 us (5%)
  between operations  13.3 us (4%)
  local copies, waits for them, and re-layouts  12.9 us (4%)
    all_gather x2, waiting for transfers between devices, piecewise(): finished.append(jax.vmap(apply)(lax.all_gather(share, axis), starts))  106 us
    dot_general x8, matrix products, attend(): jnp.einsum('hgqk,khd->hgqd', weights.astype(jnp.bfloat16), value_part, pr...  65 us
    all_gather x1, waiting for transfers between devices, per_device(): piece = lax.all_gather(key_value_pair, 'grp', axis=0, tiled=True)  52.6 us
    reduce_sum x8, other arithmetic, attend(): totals = totals * factor + jnp.sum(weights, axis=-1)  42.5 us
    dot_general x8, matrix products, attend(): jnp.einsum('qhgd,khd->hgqk', queries, key_part, preferred_element_type=jn...  28.7 us
    all_to_all x1, blocking collectives, per_device(): lax.all_to_all(attended, 'sp', split_axis=0, concat_axis=1, tiled=True)  16.4 us
    dot_general x2, matrix products, project(): return jnp.dot(piece, joined, preferred_element_type=jnp.float32)  9.01 us
  transfers between devices with their start and end apart: 3, of which 3 were waited for; matrix products, arithmetic and copies ran while one was open for 2% of the time, Pallas kernels for 0%

commit v1 on v0

--- a/solution.py
+++ b/solution.py
@@ -128,7 +128,9 @@
         jnp.ones((head_count, query_sharing, group_rows), jnp.float32),
         jnp.zeros((head_count, query_sharing, group_rows, HEAD_SIZE), jnp.float32),
     )
-    piece = lax.all_gather(key_value_pair, "grp", axis=0, tiled=True)
+    piece = jnp.concatenate(
+        lax.all_to_all(jnp.stack([key_value_pair] * lax.axis_size("grp")), "grp", 0, 0), axis=0
+    )
     step_rows = min(piece.shape[0], group_rows)
     turns = piece.shape[0] // step_rows
 

time: 354 us -> 408 us (1.15)
  waiting for transfers between devices: 160 us -> 203 us
  starting transfers between devices: 0.08 us -> 6.78 us
    all_to_all x0 -> x1, waiting for transfers between devices: none -> 96.2 us  [per_device(): lax.all_to_all(jnp.stack([key_value_pair] * lax.axis_size('grp')), 'grp',...]
    all_gather x1 -> x0, waiting for transfers between devices: 52.6 us -> none  [per_device(): piece = lax.all_gather(key_value_pair, 'grp', axis=0, tiled=True)]
    all_to_all x0 -> x1, starting transfers between devices: none -> 6.74 us  [per_device(): lax.all_to_all(jnp.stack([key_value_pair] * lax.axis_size('grp')), 'grp',...]
    dot_general x8, matrix products: 28.7 us -> 32.8 us  [attend(): jnp.einsum('qhgd,khd->hgqk', queries, key_part, preferred_element_type=jn...]
where the time goes in v1:
time: 408 us
  waiting for transfers between devices  203 us (50%)
  matrix products  107 us (26%)
  other arithmetic  46.8 us (11%)
  local copies, waits for them, and re-layouts  15.6 us (4%)
  blocking collectives  13.6 us (3%)
  between operations  13.6 us (3%)
  starting transfers between devices  6.78 us (2%)
    all_gather x2, waiting for transfers between devices, piecewise(): finished.append(jax.vmap(apply)(lax.all_gather(share, axis), starts))  106 us
    all_to_all x1, waiting for transfers between devices, per_device(): lax.all_to_all(jnp.stack([key_value_pair] * lax.axis_size('grp')), 'grp',...  96.2 us
    dot_general x8, matrix products, attend(): jnp.einsum('hgqk,khd->hgqd', weights.astype(jnp.bfloat16), value_part, pr...  65.4 us
    reduce_sum x8, other arithmetic, attend(): totals = totals * factor + jnp.sum(weights, axis=-1)  42.5 us
    dot_general x8, matrix products, attend(): jnp.einsum('qhgd,khd->hgqk', queries, key_part, preferred_element_type=jn...  32.8 us
    all_to_all x1, blocking collectives, per_device(): lax.all_to_all(attended, 'sp', split_axis=0, concat_axis=1, tiled=True)  13.6 us
    dot_general x2, matrix products, project(): return jnp.dot(piece, joined, preferred_element_type=jnp.float32)  9.01 us
  transfers between devices with their start and end apart: 3, of which 3 were waited for; matrix products, arithmetic and copies ran while one was open for 2% of the time, Pallas kernels for 0%

profile of v1, /device:TPU:1, one launch (start us, length us, event | category | flops | bytes accessed | tf_op | source)
XLA Modules:
  0.0 407.5 jit_solution(3602182995603889070)
XLA Ops:
  11.8 55.8 %all-gather.5.cloned.1.call-done = bf16[1024,2880]{1,0:T(8,128)(2,1)} async-done(((bf16[32,2880]{1,0:T(8,128)(2,1)}), bf16[1024,2880]{1,0:T(8,128)(2,1)}) %all-gather.5.cloned.1.call-update) | async-done | bytes 5898256 | tf_op jit(solution)/shard_map/all_gather | solution.py:26
  67.6 4.5 %convolution_bitcast_fusion.1 = f32[32,32,192]{2,1,0:T(8,128)S(1)} fusion(bf16[32,32,2880]{2,1,0:T(8,128)(2,1)} %bitcast.95, bf16[2880,64]{0,1:T(8,128)(2,1)S(1)} %copy.43, bf16[2880,64]{0,1:T(8,128)(2,1)S(1)} %copy.42, bf16[2880,64]{0,1:T(8,128)(2,1)S(1)} %copy-done.2), kind=kOutput, calls=%fused_computation.49 | convolution fusion | flops 1135779840 | bytes 7790592 | tf_op jit(solution)/shard_map/vmap()/dot_general | solution.py:113
  72.1 50.5 %all-gather.7.cloned.1.call-done = bf16[1024,2880]{1,0:T(8,128)(2,1)} async-done(((bf16[32,2880]{1,0:T(8,128)(2,1)}), bf16[1024,2880]{1,0:T(8,128)(2,1)}) %all-gather.7.cloned.1.call-update) | async-done | bytes 5898256 | tf_op jit(solution)/shard_map/all_gather | solution.py:26
  122.6 4.5 %convolution_bitcast_fusion = f32[32,32,192]{2,1,0:T(8,128)S(1)} fusion(bf16[32,32,2880]{2,1,0:T(8,128)(2,1)} %bitcast.96, bf16[2880,64]{0,1:T(8,128)(2,1)S(1)} %copy.43, bf16[2880,64]{0,1:T(8,128)(2,1)S(1)} %copy.42, bf16[2880,64]{0,1:T(8,128)(2,1)S(1)} %copy-done.2), kind=kOutput, calls=%fused_computation.48 | convolution fusion | flops 1135779840 | bytes 7790592 | tf_op jit(solution)/shard_map/vmap()/dot_general | solution.py:113
  132.7 6.7 %all-to-all-start = ((bf16[8,2048,128]{2,1,0:T(8,128)(2,1)}), bf16[8,2048,128]{2,1,0:T(8,128)(2,1)}, u32[]{:S(2)}, u32[]{:S(2)}) async-start(bf16[8,2048,128]{2,1,0:T(8,128)(2,1)} %stack.2), calls=%async_computation | async-start | bytes 8388608 | tf_op jit(solution)/shard_map/all_to_all | solution.py:132
  140.0 96.2 %all-to-all-done = bf16[8,2048,128]{2,1,0:T(8,128)(2,1)} async-done(((bf16[8,2048,128]{2,1,0:T(8,128)(2,1)}), bf16[8,2048,128]{2,1,0:T(8,128)(2,1)}, u32[]{:S(2)}, u32[]{:S(2)}) %all-to-all-start) | async-done | bytes 4194336 | tf_op jit(solution)/shard_map/all_to_all | solution.py:132
  236.9 146.0 %while.21 = (s32[]{:T(128)}, f32[1,1,2048]{2,1,0:T(1,128)S(1)}, f32[1,1,2048]{2,1,0:T(1,128)S(1)}, f32[1,1,2048,64]{2,3,1,0:T(8,128)S(1)}, s32[32]{0:T(128)S(1)}...) while((s32[]{:T(128)}, f32[1,1,2048]{2,1,0:T(1,128)S(1)}, ...), condition=%wide.region_5.6_spmd.clone, body=%wide.region_1.5_spmd.clone.sunk | while | flops 1141592064 | bytes 120021352 | solution.py:145
  241.2 5.3 %fusion.75 = f32[2048]{0:T(1024)S(1)} fusion(f32[2048,2048]{1,0:T(8,128)S(1)} %get-tuple-element.361, f32[2048]{0:T(1024)S(1)} %bitcast.87, s32[2048]{0:T(1024)S(1)} %get-tuple-element.395, s32[2048]{0:T(1024)S(1)} %fusion.73), kind=kLoop, calls=%fused_computation.4.clone.1 | loop fusion | flops 25163776 | bytes 16809984 | tf_op jit(solution)/shard_map/while/body/eval_jaxpr/reduce_sum | solution.py:83
  246.9 8.2 %fusion.77 = f32[1,1,2048,64]{2,3,1,0:T(8,128)S(1)} fusion(f32[2048,2048]{1,0:T(8,128)} %copy-done, f32[2048]{0:T(1024)S(1)} %bitcast.88, s32[2048]{0:T(1024)S(1)} %get-tuple-element.395, s32[2048]{0:T(1024)S(1)} %fusion.73, bf16[16384,128]{1,0:T(8,128)(2,1)} %get-tuple-element.396, s32[]{:T(128)S(6)} %select_n.248, s32[]{:T(128)S(6)} %add.421, ...), kind=kOutput, calls=%fused_computation.8.clone.1 | convolution fusion | flops 562429952 | bytes 18382856 | tf_op jit(solution)/shard_map/while/body/eval_jaxpr/hgqk,khd->hgqd/dot_general | solution.py:84
  259.4 5.3 %fusion.75 = f32[2048]{0:T(1024)S(1)} fusion(f32[2048,2048]{1,0:T(8,128)S(1)} %get-tuple-element.361, f32[2048]{0:T(1024)S(1)} %bitcast.87, s32[2048]{0:T(1024)S(1)} %get-tuple-element.395, s32[2048]{0:T(1024)S(1)} %fusion.73), kind=kLoop, calls=%fused_computation.4.clone.1 | loop fusion | flops 25163776 | bytes 16809984 | tf_op jit(solution)/shard_map/while/body/eval_jaxpr/reduce_sum | solution.py:83
  265.2 8.2 %fusion.77 = f32[1,1,2048,64]{2,3,1,0:T(8,128)S(1)} fusion(f32[2048,2048]{1,0:T(8,128)} %copy-done, f32[2048]{0:T(1024)S(1)} %bitcast.88, s32[2048]{0:T(1024)S(1)} %get-tuple-element.395, s32[2048]{0:T(1024)S(1)} %fusion.73, bf16[16384,128]{1,0:T(8,128)(2,1)} %get-tuple-element.396, s32[]{:T(128)S(6)} %select_n.248, s32[]{:T(128)S(6)} %add.421, ...), kind=kOutput, calls=%fused_computation.8.clone.1 | convolution fusion | flops 562429952 | bytes 18382856 | tf_op jit(solution)/shard_map/while/body/eval_jaxpr/hgqk,khd->hgqd/dot_general | solution.py:84
  277.7 5.3 %fusion.75 = f32[2048]{0:T(1024)S(1)} fusion(f32[2048,2048]{1,0:T(8,128)S(1)} %get-tuple-element.361, f32[2048]{0:T(1024)S(1)} %bitcast.87, s32[2048]{0:T(1024)S(1)} %get-tuple-element.395, s32[2048]{0:T(1024)S(1)} %fusion.73), kind=kLoop, calls=%fused_computation.4.clone.1 | loop fusion | flops 25163776 | bytes 16809984 | tf_op jit(solution)/shard_map/while/body/eval_jaxpr/reduce_sum | solution.py:83
  283.4 8.2 %fusion.77 = f32[1,1,2048,64]{2,3,1,0:T(8,128)S(1)} fusion(f32[2048,2048]{1,0:T(8,128)} %copy-done, f32[2048]{0:T(1024)S(1)} %bitcast.88, s32[2048]{0:T(1024)S(1)} %get-tuple-element.395, s32[2048]{0:T(1024)S(1)} %fusion.73, bf16[16384,128]{1,0:T(8,128)(2,1)} %get-tuple-element.396, s32[]{:T(128)S(6)} %select_n.248, s32[]{:T(128)S(6)} %add.421, ...), kind=kOutput, calls=%fused_computation.8.clone.1 | convolution fusion | flops 562429952 | bytes 18382856 | tf_op jit(solution)/shard_map/while/body/eval_jaxpr/hgqk,khd->hgqd/dot_general | solution.py:84
  296.0 5.3 %fusion.75 = f32[2048]{0:T(1024)S(1)} fusion(f32[2048,2048]{1,0:T(8,128)S(1)} %get-tuple-element.361, f32[2048]{0:T(1024)S(1)} %bitcast.87, s32[2048]{0:T(1024)S(1)} %get-tuple-element.395, s32[2048]{0:T(1024)S(1)} %fusion.73), kind=kLoop, calls=%fused_computation.4.clone.1 | loop fusion | flops 25163776 | bytes 16809984 | tf_op jit(solution)/shard_map/while/body/eval_jaxpr/reduce_sum | solution.py:83
  301.7 8.2 %fusion.77 = f32[1,1,2048,64]{2,3,1,0:T(8,128)S(1)} fusion(f32[2048,2048]{1,0:T(8,128)} %copy-done, f32[2048]{0:T(1024)S(1)} %bitcast.88, s32[2048]{0:T(1024)S(1)} %get-tuple-element.395, s32[2048]{0:T(1024)S(1)} %fusion.73, bf16[16384,128]{1,0:T(8,128)(2,1)} %get-tuple-element.396, s32[]{:T(128)S(6)} %select_n.248, s32[]{:T(128)S(6)} %add.421, ...), kind=kOutput, calls=%fused_computation.8.clone.1 | convolution fusion | flops 562429952 | bytes 18382856 | tf_op jit(solution)/shard_map/while/body/eval_jaxpr/hgqk,khd->hgqd/dot_general | solution.py:84
  314.2 5.3 %fusion.75 = f32[2048]{0:T(1024)S(1)} fusion(f32[2048,2048]{1,0:T(8,128)S(1)} %get-tuple-element.361, f32[2048]{0:T(1024)S(1)} %bitcast.87, s32[2048]{0:T(1024)S(1)} %get-tuple-element.395, s32[2048]{0:T(1024)S(1)} %fusion.73), kind=kLoop, calls=%fused_computation.4.clone.1 | loop fusion | flops 25163776 | bytes 16809984 | tf_op jit(solution)/shard_map/while/body/eval_jaxpr/reduce_sum | solution.py:83
  319.9 8.2 %fusion.77 = f32[1,1,2048,64]{2,3,1,0:T(8,128)S(1)} fusion(f32[2048,2048]{1,0:T(8,128)} %copy-done, f32[2048]{0:T(1024)S(1)} %bitcast.88, s32[2048]{0:T(1024)S(1)} %get-tuple-element.395, s32[2048]{0:T(1024)S(1)} %fusion.73, bf16[16384,128]{1,0:T(8,128)(2,1)} %get-tuple-element.396, s32[]{:T(128)S(6)} %select_n.248, s32[]{:T(128)S(6)} %add.421, ...), kind=kOutput, calls=%fused_computation.8.clone.1 | convolution fusion | flops 562429952 | bytes 18382856 | tf_op jit(solution)/shard_map/while/body/eval_jaxpr/hgqk,khd->hgqd/dot_general | solution.py:84
  332.5 5.3 %fusion.75 = f32[2048]{0:T(1024)S(1)} fusion(f32[2048,2048]{1,0:T(8,128)S(1)} %get-tuple-element.361, f32[2048]{0:T(1024)S(1)} %bitcast.87, s32[2048]{0:T(1024)S(1)} %get-tuple-element.395, s32[2048]{0:T(1024)S(1)} %fusion.73), kind=kLoop, calls=%fused_computation.4.clone.1 | loop fusion | flops 25163776 | bytes 16809984 | tf_op jit(solution)/shard_map/while/body/eval_jaxpr/reduce_sum | solution.py:83
  338.2 8.2 %fusion.77 = f32[1,1,2048,64]{2,3,1,0:T(8,128)S(1)} fusion(f32[2048,2048]{1,0:T(8,128)} %copy-done, f32[2048]{0:T(1024)S(1)} %bitcast.88, s32[2048]{0:T(1024)S(1)} %get-tuple-element.395, s32[2048]{0:T(1024)S(1)} %fusion.73, bf16[16384,128]{1,0:T(8,128)(2,1)} %get-tuple-element.396, s32[]{:T(128)S(6)} %select_n.248, s32[]{:T(128)S(6)} %add.421, ...), kind=kOutput, calls=%fused_computation.8.clone.1 | convolution fusion | flops 562429952 | bytes 18382856 | tf_op jit(solution)/shard_map/while/body/eval_jaxpr/hgqk,khd->hgqd/dot_general | solution.py:84
  350.7 5.3 %fusion.75 = f32[2048]{0:T(1024)S(1)} fusion(f32[2048,2048]{1,0:T(8,128)S(1)} %get-tuple-element.361, f32[2048]{0:T(1024)S(1)} %bitcast.87, s32[2048]{0:T(1024)S(1)} %get-tuple-element.395, s32[2048]{0:T(1024)S(1)} %fusion.73), kind=kLoop, calls=%fused_computation.4.clone.1 | loop fusion | flops 25163776 | bytes 16809984 | tf_op jit(solution)/shard_map/while/body/eval_jaxpr/reduce_sum | solution.py:83
  356.4 8.2 %fusion.77 = f32[1,1,2048,64]{2,3,1,0:T(8,128)S(1)} fusion(f32[2048,2048]{1,0:T(8,128)} %copy-done, f32[2048]{0:T(1024)S(1)} %bitcast.88, s32[2048]{0:T(1024)S(1)} %get-tuple-element.395, s32[2048]{0:T(1024)S(1)} %fusion.73, bf16[16384,128]{1,0:T(8,128)(2,1)} %get-tuple-element.396, s32[]{:T(128)S(6)} %select_n.248, s32[]{:T(128)S(6)} %add.421, ...), kind=kOutput, calls=%fused_computation.8.clone.1 | convolution fusion | flops 562429952 | bytes 18382856 | tf_op jit(solution)/shard_map/while/body/eval_jaxpr/hgqk,khd->hgqd/dot_general | solution.py:84
  369.0 5.3 %fusion.75 = f32[2048]{0:T(1024)S(1)} fusion(f32[2048,2048]{1,0:T(8,128)S(1)} %get-tuple-element.361, f32[2048]{0:T(1024)S(1)} %bitcast.87, s32[2048]{0:T(1024)S(1)} %get-tuple-element.395, s32[2048]{0:T(1024)S(1)} %fusion.73), kind=kLoop, calls=%fused_computation.4.clone.1 | loop fusion | flops 25163776 | bytes 16809984 | tf_op jit(solution)/shard_map/while/body/eval_jaxpr/reduce_sum | solution.py:83
  374.7 8.2 %fusion.77 = f32[1,1,2048,64]{2,3,1,0:T(8,128)S(1)} fusion(f32[2048,2048]{1,0:T(8,128)} %copy-done, f32[2048]{0:T(1024)S(1)} %bitcast.88, s32[2048]{0:T(1024)S(1)} %get-tuple-element.395, s32[2048]{0:T(1024)S(1)} %fusion.73, bf16[16384,128]{1,0:T(8,128)(2,1)} %get-tuple-element.396, s32[]{:T(128)S(6)} %select_n.248, s32[]{:T(128)S(6)} %add.421, ...), kind=kOutput, calls=%fused_computation.8.clone.1 | convolution fusion | flops 562429952 | bytes 18382856 | tf_op jit(solution)/shard_map/while/body/eval_jaxpr/hgqk,khd->hgqd/dot_general | solution.py:84
  385.2 13.6 %all_to_all.21 = bf16[32,2,2048]{2,1,0:T(2,128)(2,1)S(1)} all-to-all(bf16[32,2,2048]{2,1,0:T(2,128)(2,1)S(1)} %reshape.446), channel_id=1, replica_groups=mesh['grp'=8,'sp'=32] {'sp'}, dimensions={0} | all-to-all | bytes 524288 | tf_op jit(solution)/shard_map/all_to_all | solution.py:148
  (115 shorter events, 53.5 us)
Async XLA Ops:
  6.5 5.1 %copy-start.1 = (s32[32]{0:T(128)S(1)}, s32[32]{0:T(128)}, u32[]{:S(2)}) copy-start(s32[32]{0:T(128)} %param.10) | copy-start | bytes 388
  6.5 61.1 %copy-start.2 = (bf16[2880,64]{0,1:T(8,128)(2,1)S(1)}, bf16[2880,64]{0,1:T(8,128)(2,1)}, u32[]{:S(2)}) copy-start(bf16[2880,64]{0,1:T(8,128)(2,1)} %param.8) | copy-start | bytes 1105924
  6.5 61.1 %all-gather.5.cloned.1.call-start = ((), (), s32[]{:S(2)}) async-start(), calls=%async_computation.2 | async-start | bytes 6217728 | tf_op jit(solution)/shard_map/all_gather | solution.py:26
  8.4 114.2 %all-gather.7.cloned.1.call-start = ((), (), s32[]{:S(2)}) async-start(), calls=%async_computation.3 | async-start | bytes 6217728 | tf_op jit(solution)/shard_map/all_gather | solution.py:26
  130.2 9.2 %copy-start.3 = (f32[32]{0:T(128)S(1)}, f32[32]{0:T(128)}, u32[]{:S(2)}) copy-start(f32[32]{0:T(128)} %param.11) | copy-start | bytes 388
  132.7 103.6 %all-to-all-start = ((bf16[8,2048,128]{2,1,0:T(8,128)(2,1)}), bf16[8,2048,128]{2,1,0:T(8,128)(2,1)}, u32[]{:S(2)}, u32[]{:S(2)}) async-start(bf16[8,2048,128]{2,1,0:T(8,128)(2,1)} %stack.2), calls=%async_computation | async-start | bytes 8388608 | tf_op jit(solution)/shard_map/all_to_all | solution.py:132
  241.2 5.7 %copy-start = (f32[2048,2048]{1,0:T(8,128)}, f32[2048,2048]{1,0:T(8,128)S(1)}, u32[]{:S(2)}) copy-start(f32[2048,2048]{1,0:T(8,128)S(1)} %get-tuple-element.361) | copy-start | bytes 50331652 | tf_op jit(solution)/shard_map/while
  259.4 5.7 %copy-start = (f32[2048,2048]{1,0:T(8,128)}, f32[2048,2048]{1,0:T(8,128)S(1)}, u32[]{:S(2)}) copy-start(f32[2048,2048]{1,0:T(8,128)S(1)} %get-tuple-element.361) | copy-start | bytes 50331652 | tf_op jit(solution)/shard_map/while
  277.7 5.7 %copy-start = (f32[2048,2048]{1,0:T(8,128)}, f32[2048,2048]{1,0:T(8,128)S(1)}, u32[]{:S(2)}) copy-start(f32[2048,2048]{1,0:T(8,128)S(1)} %get-tuple-element.361) | copy-start | bytes 50331652 | tf_op jit(solution)/shard_map/while
  295.9 5.7 %copy-start = (f32[2048,2048]{1,0:T(8,128)}, f32[2048,2048]{1,0:T(8,128)S(1)}, u32[]{:S(2)}) copy-start(f32[2048,2048]{1,0:T(8,128)S(1)} %get-tuple-element.361) | copy-start | bytes 50331652 | tf_op jit(solution)/shard_map/while
  314.2 5.7 %copy-start = (f32[2048,2048]{1,0:T(8,128)}, f32[2048,2048]{1,0:T(8,128)S(1)}, u32[]{:S(2)}) copy-start(f32[2048,2048]{1,0:T(8,128)S(1)} %get-tuple-element.361) | copy-start | bytes 50331652 | tf_op jit(solution)/shard_map/while
  332.4 5.7 %copy-start = (f32[2048,2048]{1,0:T(8,128)}, f32[2048,2048]{1,0:T(8,128)S(1)}, u32[]{:S(2)}) copy-start(f32[2048,2048]{1,0:T(8,128)S(1)} %get-tuple-element.361) | copy-start | bytes 50331652 | tf_op jit(solution)/shard_map/while
  350.7 5.7 %copy-start = (f32[2048,2048]{1,0:T(8,128)}, f32[2048,2048]{1,0:T(8,128)S(1)}, u32[]{:S(2)}) copy-start(f32[2048,2048]{1,0:T(8,128)S(1)} %get-tuple-element.361) | copy-start | bytes 50331652 | tf_op jit(solution)/shard_map/while
  368.9 5.7 %copy-start = (f32[2048,2048]{1,0:T(8,128)}, f32[2048,2048]{1,0:T(8,128)S(1)}, u32[]{:S(2)}) copy-start(f32[2048,2048]{1,0:T(8,128)S(1)} %get-tuple-element.361) | copy-start | bytes 50331652 | tf_op jit(solution)/shard_map/while
Sparse Core Ops, SparseCore 0:
  9.9 57.7 all-gather.4
  70.2 52.4 all-gather.6
